TPU v7x, 32 devices: a whole 2x2x4 slice. The times are simulated.
32 devices in a mesh: px: 4 (over y, x), py: 8 (over z, core).
Axes of the slice: x: 2, y: 2, z: 4, core: 2. Of those that a mesh axis runs over, the one named last changes fastest.
Arguments:
- photons: float32 [1024, 128], P(('px', 'py')), may hold values from 50 to 1000
- halo_cells: int32 [1024, 128], P(('px', 'py')), may hold values from 0 to 1769471
- halo_counts: int32 [1024], P(('px', 'py')), may hold values from 1 to 128
- owners: int32 [1024, 1], P(('px', 'py')), may hold values from 0 to 7; in each aligned block of 32 rows (0 to 31, 32 to 63, ...) at most 4 rows name the same one
- density: float32 [384, 384, 384], P('px', 'py'), may hold values from 0.02 to 50
Outputs:
- fraction: float32 [384, 384, 384], P('px', 'py')
Inputs may be any that keep to these rules, and one draw needn't show every extreme that they name: The halos of a block all lie in pencil owners[b] of the block's own slab. Among the 32 blocks of one device no owner appears more than 4 times, a bound that some block reaches. Slots at or past halo_counts[b] are not live and carry arbitrary values. `halo_cells`: A cell index within the owner pencil is (x * 48 + y) * 384 + z with x, y, z local to that pencil.
All inputs are finite; a program needn't handle non-finite values.
Results may differ from a plain program's by a relative error of at most 0.0003.
Values sent between devices are 32-bit elements; how exact they have to be, the bound alone decides.
A program may use at most 192 MiB of HBM per device.

v0:
```python
import jax
import jax.numpy as jnp
from jax import lax
from jax.sharding import PartitionSpec as P

NG = 384
SLOTS = 128
RADIUS = 20


def product(form, left, right):
    return jnp.einsum(form, left, right, precision=lax.Precision.HIGHEST)


def rotate(form, real_part, imag_part, cos_table, sin_table, direction):
    signed_sin = direction * sin_table
    first = product(form, real_part + imag_part, cos_table)
    second = product(form, real_part, signed_sin - cos_table)
    third = product(form, imag_part, cos_table + signed_sin)
    return (first - third, first + second)


def tables(length):
    index_row = jnp.arange(length, dtype=jnp.int32)
    angle = (index_row[:, None] * index_row[None, :] % length).astype(jnp.float32) * (
        2.0 * jnp.pi / length
    )
    return (jnp.cos(angle), jnp.sin(angle))


def signed_frequency(index_values):
    return jnp.where(index_values < NG // 2, index_values, index_values - NG).astype(jnp.float32)


def top_hat(freq_x, freq_y, freq_z):
    radial = jnp.sqrt(freq_x * freq_x + freq_y * freq_y + freq_z * freq_z) * (
        2.0 * jnp.pi * RADIUS / NG
    )
    safe = jnp.where(radial > 0, radial, 1.0)
    value = 3.0 * (jnp.sin(safe) - safe * jnp.cos(safe)) / (safe * safe * safe)
    return jnp.where(radial > 0, value, 1.0)


def paint(photon_rows, cell_rows, live_rows, cell_total):
    weights = jnp.where(live_rows, photon_rows, 0.0)
    empty = jnp.zeros((cell_total,), jnp.float32)
    return empty.at[cell_rows.reshape(-1)].add(weights.reshape(-1))


def on_device(photons, halo_cells, halo_counts, owners, density):
    rows_x, rows_y = (density.shape[0], density.shape[1])
    cell_total = rows_x * rows_y * NG
    count_x = lax.axis_size("px")
    count_y = lax.axis_size("py")
    place_y = lax.axis_index("py")
    slot_index = jnp.arange(SLOTS, dtype=jnp.int32)[None, :]
    all_photons, all_cells, all_counts, all_owners = (
        lax.all_gather(photons, "py", axis=0, tiled=True),
        lax.all_gather(halo_cells, "py", axis=0, tiled=True),
        lax.all_gather(halo_counts, "py", axis=0, tiled=True),
        lax.all_gather(owners, "py", axis=0, tiled=True),
    )
    live_rows = (slot_index < all_counts[:, None]) & (all_owners == place_y)
    painted = paint(all_photons, all_cells, live_rows, cell_total)
    cos_full, sin_full = tables(NG)
    field_rows = painted.reshape(rows_x * rows_y, NG)
    density_rows = density.reshape(rows_x * rows_y, NG)
    spec_real, spec_imag = rotate("az,zk->ka", field_rows, density_rows, cos_full, sin_full, -1.0)
    cos_y = cos_full.reshape(count_y, rows_y, NG)
    sin_y = sin_full.reshape(count_y, rows_y, NG)
    cos_x = cos_full.reshape(count_x, rows_x, NG)
    sin_x = sin_full.reshape(count_x, rows_x, NG)
    freq_all = signed_frequency(jnp.arange(NG, dtype=jnp.int32))
    devices_all = count_x * count_y
    slab_planes = NG // devices_all
    sent = (
        spec_real.reshape(devices_all, slab_planes, rows_x * rows_y),
        spec_imag.reshape(devices_all, slab_planes, rows_x * rows_y),
    )
    got_real, got_imag = (
        lax.all_to_all(sent[0], ("px", "py"), split_axis=0, concat_axis=2, tiled=True),
        lax.all_to_all(sent[1], ("px", "py"), split_axis=0, concat_axis=2, tiled=True),
    )
    got_real = got_real.reshape(slab_planes, count_x, count_y, rows_x, rows_y)
    got_imag = got_imag.reshape(slab_planes, count_x, count_y, rows_x, rows_y)
    plane_real, plane_imag = rotate("kiqxl,qlm->kixm", got_real, got_imag, cos_y, sin_y, -1.0)
    full_real, full_imag = rotate("kixm,ixn->kmn", plane_real, plane_imag, cos_x, sin_x, -1.0)
    freq_z = signed_frequency(
        lax.axis_index(("px", "py")) * slab_planes + jnp.arange(slab_planes, dtype=jnp.int32)
    )
    window = top_hat(freq_z[:, None, None], freq_all[None, :, None], freq_all[None, None, :])
    full_real = full_real * window
    full_imag = full_imag * window
    plane_real, plane_imag = rotate("kmn,ixn->kmix", full_real, full_imag, cos_x, sin_x, 1.0)
    back_real, back_imag = rotate("kmix,qlm->iqkxl", plane_real, plane_imag, cos_y, sin_y, 1.0)
    sent = (
        back_real.reshape(devices_all, slab_planes, rows_x * rows_y),
        back_imag.reshape(devices_all, slab_planes, rows_x * rows_y),
    )
    got_real, got_imag = (
        lax.all_to_all(sent[0], ("px", "py"), split_axis=0, concat_axis=1, tiled=True),
        lax.all_to_all(sent[1], ("px", "py"), split_axis=0, concat_axis=1, tiled=True),
    )
    got_real = got_real.reshape(NG, rows_x * rows_y)
    got_imag = got_imag.reshape(NG, rows_x * rows_y)
    final_real, final_imag = rotate("ka,kz->az", got_real, got_imag, cos_full, sin_full, 1.0)
    scale = 1.0 / (float(NG) * float(NG) * float(NG))
    photon_smooth = final_real * scale
    density_smooth = final_imag * scale
    fraction = jnp.clip(photon_smooth / jnp.maximum(density_smooth, 0.5), 0.0, 1.0)
    return fraction.reshape(rows_x, rows_y, NG)


def solution(mesh):
    placed = (
        P(("px", "py"), None),
        P(("px", "py"), None),
        P(("px", "py")),
        P(("px", "py"), None),
        P("px", "py", None),
    )
    return jax.shard_map(
        on_device, mesh=mesh, in_specs=placed, out_specs=P("px", "py", None), check_vma=False
    )
```

profile of v0, /device:TPU:0, one launch (start us, length us, event | category | flops | bytes accessed | tf_op | source)
XLA Modules:
  0.0 1580.6 jit_solution(1984231770731450605)
XLA Ops:
  0.0 15.9 %all_gather.15 = f32[256,128]{1,0:T(8,128)S(1)} all-gather(f32[32,128]{1,0:T(8,128)} %param.5), channel_id=1, replica_groups=mesh['px'=4,'py'=8] {'py'}, dimensions={0}, use_global_device_ids=true | all-gather | bytes 147456 | tf_op jit(solution)/shard_map/all_gather | solution.py:58
  15.9 14.2 all_gather.12
  42.8 174.8 %scatter_custom_fusion = f32[1769472]{0:T(1024)} fusion(s32[32768]{0:T(1024)S(1)} %bitcast.192, f32[32768]{0:T(1024)S(1)} %select_bitcast_fusion, f32[]{:T(128)} %constant.19.clone.1), kind=kCustom, calls=%fused_computation.47 | custom fusion | flops 32768 | bytes 7077892 | tf_op jit(solution)/shard_map/scatter-add | solution.py:47
  226.4 24.8 %fusion.29 = f32[384,4608]{1,0:T(8,128)S(1)} fusion(f32[4608,384]{1,0:T(8,128)} %reshape.184, f32[4608,384]{1,0:T(8,128)} %bitcast.189), kind=kOutput, calls=%fused_computation.45 | convolution fusion | flops 8156823552 | bytes 21233664 | tf_op jit(solution)/shard_map/az,zk->ka/dot_general | solution.py:12
  254.1 26.1 %convolution_add_fusion.1 = f32[384,4608]{1,0:T(8,128)} fusion(f32[384,4608]{1,0:T(8,128)S(1)} %fusion.29, f32[4608,384]{1,0:T(8,128)S(1)} %copy-done.6), kind=kOutput, calls=%fused_computation.11 | convolution fusion | flops 8157118464 | bytes 21233664 | tf_op jit(solution)/shard_map/az,zk->ka/dot_general | solution.py:12
  292.1 29.4 %convolution_subtract_fusion.1 = f32[384,4608]{1,0:T(8,128)} fusion(f32[384,4608]{1,0:T(8,128)} %copy-done.3, f32[4608,384]{1,0:T(8,128)} %bitcast.190), kind=kOutput, calls=%fused_computation.12 | convolution fusion | flops 8157118464 | bytes 21233664 | tf_op jit(solution)/shard_map/az,zk->ka/dot_general | solution.py:12
  329.5 169.9 %all-to-all-done.1 = f32[32,12,4608]{2,1,0:T(8,128)} async-done(((f32[32,12,4608]{2,1,0:T(8,128)}), f32[32,12,4608]{2,1,0:T(8,128)}, u32[]{:S(2)}, u32[]{:S(2)}) %all-to-all-start.1) | async-done | bytes 7077920 | tf_op jit(solution)/shard_map/all_to_all | solution.py:82
  508.5 10.7 copy.16
  519.2 26.0 %reshape.189 = f32[12,4,8,96,48]{4,3,2,1,0:T(8,128)} reshape(f32[1,12,32,4608]{3,2,1,0:T(8,128)} %copy.16) | data formatting | bytes 14155776 | tf_op jit(solution)/shard_map/reshape | solution.py:85
  545.3 165.4 %all-to-all-done = f32[32,12,4608]{2,1,0:T(8,128)} async-done(((f32[32,12,4608]{2,1,0:T(8,128)}), f32[32,12,4608]{2,1,0:T(8,128)}, u32[]{:S(2)}, u32[]{:S(2)}) %all-to-all-start) | async-done | bytes 7077920 | tf_op jit(solution)/shard_map/all_to_all | solution.py:81
  721.4 15.1 reshape.187
  736.5 26.2 %fusion.53 = f32[12,4,96,384,1]{3,2,4,1,0:T(8,128)} fusion(f32[12,4,8,96,48]{4,3,2,1,0:T(8,128)} %reshape.189, s32[8,48]{1,0:T(8,128)S(1)} %multiply_add_fusion), kind=kOutput, calls=%fused_computation.69 | convolution fusion | flops 8155348992 | bytes 14157312 | tf_op jit(solution)/shard_map/kiqxl,qlm->kixm/dot_general | solution.py:12
  762.7 27.8 %fusion = f32[12,4,96,384,1]{3,2,4,1,0:T(8,128)} fusion(f32[12,4,8,96,48]{4,3,2,1,0:T(8,128)S(1)} %copy-done, f32[12,4,8,96,48]{4,3,2,1,0:T(8,128)} %reshape.189, s32[8,48]{1,0:T(8,128)S(1)} %multiply_add_fusion), kind=kOutput, calls=%fused_computation.1 | convolution fusion | flops 8156823552 | bytes 21235200 | tf_op jit(solution)/shard_map/kiqxl,qlm->kixm/dot_general | solution.py:12
  790.5 22.9 %fusion.51 = f32[12,4,96,384,1]{3,2,4,1,0:T(8,128)} fusion(f32[12,4,8,96,48]{4,3,2,1,0:T(8,128)S(1)} %copy-done, s32[8,48]{1,0:T(8,128)S(1)} %multiply_add_fusion), kind=kOutput, calls=%fused_computation.67 | convolution fusion | flops 8155348992 | bytes 14157312 | tf_op jit(solution)/shard_map/kiqxl,qlm->kixm/dot_general | solution.py:12
  813.4 25.1 %fusion.27 = f32[12,384,384,1]{2,1,3,0:T(8,128)S(1)} fusion(f32[12,4,96,384,1]{3,2,4,1,0:T(8,128)} %fusion.53, f32[12,4,96,384,1]{3,2,4,1,0:T(8,128)} %fusion, f32[12,4,96,384,1]{3,2,4,1,0:T(8,128)} %fusion.51, s32[4,96]{1,0:T(4,128)S(1)} %multiply_add_fusion.1), kind=kOutput, calls=%fused_computation.43 | convolution fusion | flops 8160362496 | bytes 28313088 | tf_op jit(solution)/shard_map/kixm,ixn->kmn/dot_general | solution.py:12
  838.5 50.9 %fusion.21 = f32[12,384,384]{2,1,0:T(8,128)S(1)} fusion(f32[12,384,384,1]{2,1,3,0:T(8,128)S(1)} %fusion.27, f32[384]{0:T(512)S(1)} %fusion.197, f32[12,384]{1,0:T(8,128)S(1)} %broadcast_add_fusion, f32[12,4,96,384,1]{3,2,4,1,0:T(8,128)} %fusion.53, f32[12,4,96,384,1]{3,2,4,1,0:T(8,128)S(1)} %copy-done.7, f32[4,96,384,1]{2,1,0,3:T(8,128)S(1)} %fusion.272), kind=kOutput, calls=%fused_computation.33 | convolution fusion | flops 8178499584 | bytes 28921344 | tf_op jit(solution)/shard_map/kixm,ixn->kmn/dot_general | solution.py:12
  889.5 20.6 %fusion.11 = f32[12,384,4,96]{1,3,2,0:T(8,128)} fusion(f32[12,384,384]{2,1,0:T(8,128)S(1)} %fusion.21, s32[4,96]{1,0:T(4,128)S(1)} %multiply_add_fusion.1), kind=kOutput, calls=%fused_computation.22 | convolution fusion | flops 8155201536 | bytes 14157312 | tf_op jit(solution)/shard_map/kmn,ixn->kmix/dot_general | solution.py:12
  910.1 50.8 %fusion.22 = f32[12,384,384]{2,1,0:T(8,128)S(1)} fusion(f32[12,384,384,1]{2,1,3,0:T(8,128)} %copy-done.9, f32[384]{0:T(512)S(1)} %fusion.197, f32[12,384]{1,0:T(8,128)S(1)} %broadcast_add_fusion, f32[12,4,96,384,1]{3,2,4,1,0:T(8,128)S(1)} %bitcast.186, f32[12,4,96,384,1]{3,2,4,1,0:T(8,128)S(1)} %copy-done.7, f32[4,96,384,1]{2,1,0,3:T(8,128)S(1)} %fusion.274), kind=kOutput, calls=%fused_computation.35 | convolution fusion | flops 8178499584 | bytes 28921344 | tf_op jit(solution)/shard_map/kixm,ixn->kmn/dot_general | solution.py:12
  963.8 14.4 fusion.13
  978.3 20.0 %fusion.9 = f32[12,384,4,96]{1,3,2,0:T(8,128)S(1)} fusion(f32[12,384,384]{2,1,0:T(8,128)} %copy-done.8, s32[4,96]{1,0:T(4,128)S(1)} %multiply_add_fusion.1), kind=kOutput, calls=%fused_computation.20 | convolution fusion | flops 8155201536 | bytes 14157312 | tf_op jit(solution)/shard_map/kmn,ixn->kmix/dot_general | solution.py:12
  998.3 24.4 %fusion.19 = f32[8,48,12,4,96]{4,1,3,2,0:T(8,128)S(1)} fusion(f32[12,384,4,96]{1,3,2,0:T(8,128)S(1)} %fusion.13, f32[12,384,4,96]{1,3,2,0:T(8,128)S(1)} %fusion.9, f32[12,384,4,96]{1,3,2,0:T(8,128)} %fusion.11, s32[8,48]{1,0:T(8,128)S(1)} %multiply_add_fusion), kind=kOutput, calls=%fused_computation.30 | convolution fusion | flops 8160362496 | bytes 28313088 | tf_op jit(solution)/shard_map/kmix,qlm->iqkxl/dot_general | solution.py:12
  1026.4 24.8 %add_bitcast_fusion = f32[4,8,12,96,48]{3,4,0,2,1:T(8,128)} fusion(f32[8,48,12,4,96]{4,1,3,2,0:T(8,128)S(1)} %fusion.19, f32[12,384,4,96]{1,3,2,0:T(8,128)S(1)} %fusion.13, f32[12,384,4,96]{1,3,2,0:T(8,128)} %fusion.11, s32[8,48]{1,0:T(8,128)S(1)} %multiply_add_fusion), kind=kOutput, calls=%fused_computation.5 | convolution fusion | flops 8158740480 | bytes 28313088 | tf_op jit(solution)/shard_map/kmix,qlm->iqkxl/dot_general | solution.py:12
  1051.2 14.8 copy.43
  1065.9 19.0 %reshape.239 = f32[32,12,4608]{2,1,0:T(8,128)} reshape(f32[4,8,12,96,48]{4,3,2,1,0:T(8,128)} %copy.43) | data formatting | bytes 14155776 | tf_op jit(solution)/shard_map/reshape | solution.py:98
  1089.1 31.1 %subtract_bitcast_fusion = f32[4,8,12,96,48]{3,4,0,2,1:T(8,128)} fusion(f32[8,48,12,4,96]{4,1,3,2,0:T(8,128)} %copy-done.4, f32[12,384,4,96]{1,3,2,0:T(8,128)} %copy-done.2, f32[12,384,4,96]{1,3,2,0:T(8,128)} %copy-done.5, s32[8,48]{1,0:T(8,128)S(1)} %multiply_add_fusion), kind=kOutput, calls=%fused_computation.6 | convolution fusion | flops 8158740480 | bytes 28313088 | tf_op jit(solution)/shard_map/kmix,qlm->iqkxl/dot_general | solution.py:12
  1120.2 14.8 copy.42
  1134.9 19.0 %reshape.238 = f32[32,12,4608]{2,1,0:T(8,128)} reshape(f32[4,8,12,96,48]{4,3,2,1,0:T(8,128)} %copy.42) | data formatting | bytes 14155776 | tf_op jit(solution)/shard_map/reshape | solution.py:97
  1154.0 142.4 %all-to-all-done.3 = f32[32,12,4608]{2,1,0:T(8,128)} async-done(((f32[32,12,4608]{2,1,0:T(8,128)}), f32[32,12,4608]{2,1,0:T(8,128)}, u32[]{:S(2)}, u32[]{:S(2)}) %all-to-all-start.3) | async-done | bytes 7077920 | tf_op jit(solution)/shard_map/all_to_all | solution.py:102
  1308.3 199.0 %all-to-all-done.2 = f32[32,12,4608]{2,1,0:T(8,128)} async-done(((f32[32,12,4608]{2,1,0:T(8,128)}), f32[32,12,4608]{2,1,0:T(8,128)}, u32[]{:S(2)}, u32[]{:S(2)}) %all-to-all-start.2) | async-done | bytes 7077920 | tf_op jit(solution)/shard_map/all_to_all | solution.py:101
  1515.5 23.8 %fusion.23 = f32[4608,384]{1,0:T(8,128)S(1)} fusion(f32[384,4608]{1,0:T(8,128)} %reshape.191, f32[384,4608]{1,0:T(8,128)} %reshape.193), kind=kOutput, calls=%fused_computation.39 | convolution fusion | flops 8156823552 | bytes 21233664 | tf_op jit(solution)/shard_map/ka,kz->az/dot_general | solution.py:12
  1539.4 18.7 %fusion.4 = f32[4608,384]{1,0:T(8,128)S(1)} fusion(f32[4608,384]{1,0:T(8,128)S(1)} %fusion.23, f32[384,4608]{1,0:T(8,128)S(1)} %copy-done.1), kind=kOutput, calls=%fused_computation.15 | convolution fusion | flops 8160509952 | bytes 21233664 | tf_op jit(solution)/shard_map/ka,kz->az/dot_general | solution.py:12
  1558.1 22.3 %divide_clamp_fusion = f32[4608,384]{1,0:T(8,128)} fusion(f32[4608,384]{1,0:T(8,128)S(1)} %fusion.4, f32[4608,384]{1,0:T(8,128)S(1)} %fusion.23, f32[384,4608]{1,0:T(8,128)S(1)} %bitcast.188), kind=kOutput, calls=%fused_computation.38 | convolution fusion | flops 8162279424 | bytes 28311552 | tf_op jit(solution)/shard_map/ka,kz->az/dot_general | solution.py:12
  (56 shorter events, 94.3 us)
Async XLA Ops:
  226.4 27.8 %copy-start.6 = (f32[4608,384]{1,0:T(8,128)S(1)}, f32[4608,384]{1,0:T(8,128)}, u32[]{:S(2)}) copy-start(f32[4608,384]{1,0:T(8,128)} %reshape.184) | copy-start | bytes 21233668
  251.2 2.9 copy-start.3
  288.2 211.2 %all-to-all-start.1 = ((f32[32,12,4608]{2,1,0:T(8,128)}), f32[32,12,4608]{2,1,0:T(8,128)}, u32[]{:S(2)}, u32[]{:S(2)}) async-start(f32[32,12,4608]{2,1,0:T(8,128)} %reshape.188), calls=%async_computation.1 | async-start | bytes 18874368 | tf_op jit(solution)/shard_map/all_to_all | solution.py:82
  499.4 211.3 %all-to-all-start = ((f32[32,12,4608]{2,1,0:T(8,128)}), f32[32,12,4608]{2,1,0:T(8,128)}, u32[]{:S(2)}, u32[]{:S(2)}) async-start(f32[32,12,4608]{2,1,0:T(8,128)} %reshape.186), calls=%async_computation | async-start | bytes 18874368 | tf_op jit(solution)/shard_map/all_to_all | solution.py:81
  736.5 26.2 %copy-start = (f32[12,4,8,96,48]{4,3,2,1,0:T(8,128)S(1)}, f32[12,4,8,96,48]{4,3,2,1,0:T(8,128)}, u32[]{:S(2)}) copy-start(f32[12,4,8,96,48]{4,3,2,1,0:T(8,128)} %reshape.187) | copy-start | bytes 21233668
  813.4 25.1 %copy-start.7 = (f32[12,4,96,384,1]{3,2,4,1,0:T(8,128)S(1)}, f32[12,4,96,384,1]{3,2,4,1,0:T(8,128)}, u32[]{:S(2)}) copy-start(f32[12,4,96,384,1]{3,2,4,1,0:T(8,128)} %fusion) | copy-start | bytes 21233668
  813.4 96.7 %slice-start = ((s8[7077888]{0:T(1024)(128)(4,1)}), s8[4194304]{0:T(1024)(128)(4,1)S(1)}, s32[]{:S(2)}) async-start(s8[7077888]{0:T(1024)(128)(4,1)} %bitcast.185), calls=%async_computation.4 | async-start | bytes 8388608
  838.5 50.9 %copy-start.9 = (f32[12,384,384,1]{2,1,3,0:T(8,128)}, f32[12,384,384,1]{2,1,3,0:T(8,128)S(1)}, u32[]{:S(2)}) copy-start(f32[12,384,384,1]{2,1,3,0:T(8,128)S(1)} %fusion.27) | copy-start | bytes 21233668
  838.5 71.6 %slice-start.1 = ((s8[7077888]{0:T(1024)(128)(4,1)}), s8[2883584]{0:T(1024)(128)(4,1)S(1)}, s32[]{:S(2)}) async-start(s8[7077888]{0:T(1024)(128)(4,1)} %bitcast.185), calls=%async_computation.5 | async-start | bytes 5767168
  960.8 3.0 copy-start.8
  978.2 44.5 %copy-start.2 = (f32[12,384,4,96]{1,3,2,0:T(8,128)}, f32[12,384,4,96]{1,3,2,0:T(8,128)S(1)}, u32[]{:S(2)}) copy-start(f32[12,384,4,96]{1,3,2,0:T(8,128)S(1)} %fusion.13) | copy-start | bytes 21233668
  998.3 24.5 %copy-start.5 = (f32[12,384,4,96]{1,3,2,0:T(8,128)}, f32[12,384,4,96]{1,3,2,0:T(8,128)S(1)}, u32[]{:S(2)}) copy-start(f32[12,384,4,96]{1,3,2,0:T(8,128)S(1)} %fusion.9) | copy-start | bytes 21233668
  1022.7 3.7 copy-start.4
  1084.9 211.4 %all-to-all-start.3 = ((f32[32,12,4608]{2,1,0:T(8,128)}), f32[32,12,4608]{2,1,0:T(8,128)}, u32[]{:S(2)}, u32[]{:S(2)}) async-start(f32[32,12,4608]{2,1,0:T(8,128)} %reshape.239), calls=%async_computation.3 | async-start | bytes 18874368 | tf_op jit(solution)/shard_map/all_to_all | solution.py:102
  1296.3 211.0 %all-to-all-start.2 = ((f32[32,12,4608]{2,1,0:T(8,128)}), f32[32,12,4608]{2,1,0:T(8,128)}, u32[]{:S(2)}, u32[]{:S(2)}) async-start(f32[32,12,4608]{2,1,0:T(8,128)} %reshape.238), calls=%async_computation.2 | async-start | bytes 18874368 | tf_op jit(solution)/shard_map/all_to_all | solution.py:101
  1515.5 23.9 %copy-start.1 = (f32[384,4608]{1,0:T(8,128)S(1)}, f32[384,4608]{1,0:T(8,128)}, u32[]{:S(2)}) copy-start(f32[384,4608]{1,0:T(8,128)} %reshape.191) | copy-start | bytes 21233668
  1515.5 42.5 %slice-start.2 = ((s8[7077888]{0:T(1024)(128)(4,1)}), s8[4194304]{0:T(1024)(128)(4,1)S(1)}, s32[]{:S(2)}) async-start(s8[7077888]{0:T(1024)(128)(4,1)} %bitcast.187), calls=%async_computation.6 | async-start | bytes 8388608
  1539.4 18.7 %slice-start.3 = ((s8[7077888]{0:T(1024)(128)(4,1)}), s8[2883584]{0:T(1024)(128)(4,1)S(1)}, s32[]{:S(2)}) async-start(s8[7077888]{0:T(1024)(128)(4,1)} %bitcast.187), calls=%async_computation.7 | async-start | bytes 5767168
where the time goes:
time: 1590 us; the launch traced here: 1580 us
  waiting for transfers between devices  677 us (43%)
  matrix products  484 us (30%)
  local copies, waits for them, and re-layouts  184 us (12%)
  other arithmetic  180 us (11%)
  blocking collectives  39 us (2%)
    dot_general x18, matrix products, product(): return jnp.einsum(form, left, right, precision=lax.Precision.HIGHEST)  484 us
    all_to_all x1, waiting for transfers between devices, on_device(): lax.all_to_all(sent[0], ('px', 'py'), split_axis=0, concat_axis=1, tiled=...  199 us
    scatter-add x1, other arithmetic, paint(): return empty.at[cell_rows.reshape(-1)].add(weights.reshape(-1))  175 us
    all_to_all x1, waiting for transfers between devices, on_device(): lax.all_to_all(sent[1], ('px', 'py'), split_axis=0, concat_axis=2, tiled=...  170 us
    all_to_all x1, waiting for transfers between devices, on_device(): lax.all_to_all(sent[0], ('px', 'py'), split_axis=0, concat_axis=2, tiled=...  165 us
    all_to_all x1, waiting for transfers between devices, on_device(): lax.all_to_all(sent[1], ('px', 'py'), split_axis=0, concat_axis=1, tiled=...  142 us
    reshape x2, local copies, waits for them, and re-layouts, on_device(): back_imag.reshape(devices_all, slab_planes, rows_x * rows_y)  33.8 us
    reshape x2, local copies, waits for them, and re-layouts, on_device(): back_real.reshape(devices_all, slab_planes, rows_x * rows_y)  33.8 us
  transfers between devices with their start and end apart: 4, of which 4 were waited for; matrix products, arithmetic and copies ran while one was open for 10% of the time, Pallas kernels for 0%

commit v1 on v0

--- a/solution.py
+++ b/solution.py
@@ -6,6 +6,13 @@
 NG = 384
 SLOTS = 128
 RADIUS = 20
+
+
+def swap_blocks(x, axis, split, join):
+    peers = lax.axis_size(axis)
+    parts = jnp.stack(jnp.split(x, peers, axis=split), axis=0)
+    parts = lax.all_to_all(parts, axis, split_axis=0, concat_axis=0)
+    return jnp.concatenate(parts, axis=join)
 
 
 def product(form, left, right):
@@ -79,7 +86,7 @@
     )
     got_real, got_imag = (
         lax.all_to_all(sent[0], ("px", "py"), split_axis=0, concat_axis=2, tiled=True),
-        lax.all_to_all(sent[1], ("px", "py"), split_axis=0, concat_axis=2, tiled=True),
+        swap_blocks(sent[1], ("px", "py"), 0, 2),
     )
     got_real = got_real.reshape(slab_planes, count_x, count_y, rows_x, rows_y)
     got_imag = got_imag.reshape(slab_planes, count_x, count_y, rows_x, rows_y)

time: 1590 us -> 1530 us (0.962)
  waiting for transfers between devices: 677 us -> 639 us
    all_to_all x1, waiting for transfers between devices: 170 us -> 119 us  [swap_blocks(): parts = lax.all_to_all(parts, axis, split_axis=0, concat_axis=0)]
    reshape x2 -> x1, local copies, waits for them, and re-layouts: 34 us -> 8.25 us  [swap_blocks(): return jnp.concatenate(parts, axis=join)]
    another operation x0 -> x3, local copies, waits for them, and re-layouts: none -> 23.6 us  [the longest x1 15.2 us: on_device(): got_imag = got_imag.reshape(slab_planes, count_x, count_y, rows_x, rows_y)]
  transfers between devices with their start and end apart: 4 -> 4, of which waited for: 4 -> 4; matrix products, arithmetic and copies ran while one was open for 10% -> 9% of each run, Pallas kernels for 0% -> 0%
where the time goes in v1:
time: 1530 us; the launch traced here: 1520 us
  waiting for transfers between devices  639 us (42%)
  matrix products  479 us (31%)
  other arithmetic  180 us (12%)
  local copies, waits for them, and re-layouts  169 us (11%)
  blocking collectives  39 us (3%)
  starting transfers between devices  15.3 us (1%)
    dot_general x18, matrix products, product(): return jnp.einsum(form, left, right, precision=lax.Precision.HIGHEST)  479 us
    all_to_all x1, waiting for transfers between devices, on_device(): lax.all_to_all(sent[0], ('px', 'py'), split_axis=0, concat_axis=1, tiled=...  199 us
    all_to_all x1, waiting for transfers between devices, on_device(): lax.all_to_all(sent[0], ('px', 'py'), split_axis=0, concat_axis=2, tiled=...  179 us
    scatter-add x1, other arithmetic, paint(): return empty.at[cell_rows.reshape(-1)].add(weights.reshape(-1))  174 us
    all_to_all x1, waiting for transfers between devices, on_device(): lax.all_to_all(sent[1], ('px', 'py'), split_axis=0, concat_axis=1, tiled=...  142 us
    all_to_all x1, waiting for transfers between devices, swap_blocks(): parts = lax.all_to_all(parts, axis, split_axis=0, concat_axis=0)  119 us
    reshape x2, local copies, waits for them, and re-layouts, on_device(): back_imag.reshape(devices_all, slab_planes, rows_x * rows_y)  33.8 us
    reshape x2, local copies, waits for them, and re-layouts, on_device(): back_real.reshape(devices_all, slab_planes, rows_x * rows_y)  33.8 us
  transfers between devices with their start and end apart: 4, of which 4 were waited for; matrix products, arithmetic and copies ran while one was open for 9% of the time, Pallas kernels for 0%

profile of v1, /device:TPU:0, one launch (start us, length us, event | category | flops | bytes accessed | tf_op | source)
XLA Modules:
  0.0 1523.1 jit_solution(17915809104628593932)
XLA Ops:
  0.0 15.9 %all_gather.15 = f32[256,128]{1,0:T(8,128)S(1)} all-gather(f32[32,128]{1,0:T(8,128)} %param.5), channel_id=1, replica_groups=mesh['px'=4,'py'=8] {'py'}, dimensions={0}, use_global_device_ids=true | all-gather | bytes 147456 | tf_op jit(solution)/shard_map/all_gather | solution.py:65
  15.9 14.2 all_gather.12
  42.8 174.5 %scatter_custom_fusion = f32[1769472]{0:T(1024)} fusion(s32[32768]{0:T(1024)S(1)} %bitcast.318, f32[32768]{0:T(1024)S(1)} %select_bitcast_fusion, f32[]{:T(128)} %constant.19.clone.1), kind=kCustom, calls=%fused_computation.47 | custom fusion | flops 32768 | bytes 7077892 | tf_op jit(solution)/shard_map/scatter-add | solution.py:54
  226.1 25.1 %fusion.29 = f32[384,4608]{1,0:T(8,128)S(1)} fusion(f32[4608,384]{1,0:T(8,128)} %reshape.245, f32[4608,384]{1,0:T(8,128)} %bitcast.315), kind=kOutput, calls=%fused_computation.45 | convolution fusion | flops 8156823552 | bytes 21233664 | tf_op jit(solution)/shard_map/az,zk->ka/dot_general | solution.py:19
  251.1 20.5 %convolution_add_fusion.1 = f32[384,4608]{1,0:T(8,128)S(1)} fusion(f32[384,4608]{1,0:T(8,128)S(1)} %fusion.29, f32[4608,384]{1,0:T(8,128)S(1)} %copy-done.6), kind=kOutput, calls=%fused_computation.11 | convolution fusion | flops 8157118464 | bytes 21233664 | tf_op jit(solution)/shard_map/az,zk->ka/dot_general | solution.py:19
  284.9 29.4 %convolution_subtract_fusion.1 = f32[384,4608]{1,0:T(8,128)} fusion(f32[384,4608]{1,0:T(8,128)} %copy-done.3, f32[4608,384]{1,0:T(8,128)} %bitcast.316), kind=kOutput, calls=%fused_computation.12 | convolution fusion | flops 8157118464 | bytes 21233664 | tf_op jit(solution)/shard_map/az,zk->ka/dot_general | solution.py:19
  322.2 119.3 %all-to-all-done.1 = f32[32,1,12,4608]{3,1,2,0:T(1,128)} async-done(((f32[32,1,12,4608]{3,1,2,0:T(1,128)}), f32[32,1,12,4608]{3,1,2,0:T(1,128)}, u32[]{:S(2)}, u32[]{:S(2)}) %all-to-all-start.1) | async-done | bytes 7077920 | tf_op jit(solution)/shard_map/all_to_all | solution.py:14
  458.9 15.2 reshape_reshape.3
  474.0 178.7 %all-to-all-done = f32[32,12,4608]{2,1,0:T(8,128)} async-done(((f32[32,12,4608]{2,1,0:T(8,128)}), f32[32,12,4608]{2,1,0:T(8,128)}, u32[]{:S(2)}, u32[]{:S(2)}) %all-to-all-start) | async-done | bytes 7077920 | tf_op jit(solution)/shard_map/all_to_all | solution.py:88
  652.7 10.7 copy.17
  663.5 15.1 reshape.248
  678.6 26.6 %fusion.53 = f32[12,4,96,384,1]{3,2,4,1,0:T(8,128)} fusion(f32[12,4,8,96,48]{4,3,2,1,0:T(8,128)} %reshape_reshape.3, s32[8,48]{1,0:T(8,128)S(1)} %multiply_add_fusion), kind=kOutput, calls=%fused_computation.69 | convolution fusion | flops 8155348992 | bytes 14157312 | tf_op jit(solution)/shard_map/kiqxl,qlm->kixm/dot_general | solution.py:19
  705.2 27.8 %fusion = f32[12,4,96,384,1]{3,2,4,1,0:T(8,128)} fusion(f32[12,4,8,96,48]{4,3,2,1,0:T(8,128)S(1)} %copy-done, f32[12,4,8,96,48]{4,3,2,1,0:T(8,128)} %reshape_reshape.3, s32[8,48]{1,0:T(8,128)S(1)} %multiply_add_fusion), kind=kOutput, calls=%fused_computation.1 | convolution fusion | flops 8156823552 | bytes 21235200 | tf_op jit(solution)/shard_map/kiqxl,qlm->kixm/dot_general | solution.py:19
  733.0 22.7 %fusion.51 = f32[12,4,96,384,1]{3,2,4,1,0:T(8,128)} fusion(f32[12,4,8,96,48]{4,3,2,1,0:T(8,128)S(1)} %copy-done, s32[8,48]{1,0:T(8,128)S(1)} %multiply_add_fusion), kind=kOutput, calls=%fused_computation.67 | convolution fusion | flops 8155348992 | bytes 14157312 | tf_op jit(solution)/shard_map/kiqxl,qlm->kixm/dot_general | solution.py:19
  755.7 25.3 %fusion.27 = f32[12,384,384,1]{2,1,3,0:T(8,128)S(1)} fusion(f32[12,4,96,384,1]{3,2,4,1,0:T(8,128)} %fusion.53, f32[12,4,96,384,1]{3,2,4,1,0:T(8,128)} %fusion, f32[12,4,96,384,1]{3,2,4,1,0:T(8,128)} %fusion.51, s32[4,96]{1,0:T(4,128)S(1)} %multiply_add_fusion.1), kind=kOutput, calls=%fused_computation.43 | convolution fusion | flops 8160362496 | bytes 28313088 | tf_op jit(solution)/shard_map/kixm,ixn->kmn/dot_general | solution.py:19
  781.0 50.9 %fusion.21 = f32[12,384,384]{2,1,0:T(8,128)S(1)} fusion(f32[12,384,384,1]{2,1,3,0:T(8,128)S(1)} %fusion.27, f32[384]{0:T(512)S(1)} %fusion.229, f32[12,384]{1,0:T(8,128)S(1)} %broadcast_add_fusion, f32[12,4,96,384,1]{3,2,4,1,0:T(8,128)} %fusion.53, f32[12,4,96,384,1]{3,2,4,1,0:T(8,128)S(1)} %copy-done.7, f32[4,96,384,1]{2,1,0,3:T(8,128)S(1)} %fusion.304), kind=kOutput, calls=%fused_computation.33 | convolution fusion | flops 8178499584 | bytes 28921344 | tf_op jit(solution)/shard_map/kixm,ixn->kmn/dot_general | solution.py:19
  832.0 20.6 %fusion.11 = f32[12,384,4,96]{1,3,2,0:T(8,128)} fusion(f32[12,384,384]{2,1,0:T(8,128)S(1)} %fusion.21, s32[4,96]{1,0:T(4,128)S(1)} %multiply_add_fusion.1), kind=kOutput, calls=%fused_computation.22 | convolution fusion | flops 8155201536 | bytes 14157312 | tf_op jit(solution)/shard_map/kmn,ixn->kmix/dot_general | solution.py:19
  852.5 50.6 %fusion.22 = f32[12,384,384]{2,1,0:T(8,128)S(1)} fusion(f32[12,384,384,1]{2,1,3,0:T(8,128)} %copy-done.9, f32[384]{0:T(512)S(1)} %fusion.229, f32[12,384]{1,0:T(8,128)S(1)} %broadcast_add_fusion, f32[12,4,96,384,1]{3,2,4,1,0:T(8,128)S(1)} %bitcast.312, f32[12,4,96,384,1]{3,2,4,1,0:T(8,128)S(1)} %copy-done.7, f32[4,96,384,1]{2,1,0,3:T(8,128)S(1)} %fusion.306), kind=kOutput, calls=%fused_computation.35 | convolution fusion | flops 8178499584 | bytes 28921344 | tf_op jit(solution)/shard_map/kixm,ixn->kmn/dot_general | solution.py:19
  906.1 14.7 fusion.13
  920.8 19.9 %fusion.9 = f32[12,384,4,96]{1,3,2,0:T(8,128)S(1)} fusion(f32[12,384,384]{2,1,0:T(8,128)} %copy-done.8, s32[4,96]{1,0:T(4,128)S(1)} %multiply_add_fusion.1), kind=kOutput, calls=%fused_computation.20 | convolution fusion | flops 8155201536 | bytes 14157312 | tf_op jit(solution)/shard_map/kmn,ixn->kmix/dot_general | solution.py:19
  940.7 24.2 %fusion.19 = f32[8,48,12,4,96]{4,1,3,2,0:T(8,128)S(1)} fusion(f32[12,384,4,96]{1,3,2,0:T(8,128)S(1)} %fusion.13, f32[12,384,4,96]{1,3,2,0:T(8,128)S(1)} %fusion.9, f32[12,384,4,96]{1,3,2,0:T(8,128)} %fusion.11, s32[8,48]{1,0:T(8,128)S(1)} %multiply_add_fusion), kind=kOutput, calls=%fused_computation.30 | convolution fusion | flops 8160362496 | bytes 28313088 | tf_op jit(solution)/shard_map/kmix,qlm->iqkxl/dot_general | solution.py:19
  968.6 25.1 %add_bitcast_fusion = f32[4,8,12,96,48]{3,4,0,2,1:T(8,128)} fusion(f32[8,48,12,4,96]{4,1,3,2,0:T(8,128)S(1)} %fusion.19, f32[12,384,4,96]{1,3,2,0:T(8,128)S(1)} %fusion.13, f32[12,384,4,96]{1,3,2,0:T(8,128)} %fusion.11, s32[8,48]{1,0:T(8,128)S(1)} %multiply_add_fusion), kind=kOutput, calls=%fused_computation.5 | convolution fusion | flops 8158740480 | bytes 28313088 | tf_op jit(solution)/shard_map/kmix,qlm->iqkxl/dot_general | solution.py:19
  993.7 14.8 copy.46
  1008.5 19.0 %reshape.299 = f32[32,12,4608]{2,1,0:T(8,128)} reshape(f32[4,8,12,96,48]{4,3,2,1,0:T(8,128)} %copy.46) | data formatting | bytes 14155776 | tf_op jit(solution)/shard_map/reshape | solution.py:105
  1031.4 31.1 %subtract_bitcast_fusion = f32[4,8,12,96,48]{3,4,0,2,1:T(8,128)} fusion(f32[8,48,12,4,96]{4,1,3,2,0:T(8,128)} %copy-done.4, f32[12,384,4,96]{1,3,2,0:T(8,128)} %copy-done.2, f32[12,384,4,96]{1,3,2,0:T(8,128)} %copy-done.5, s32[8,48]{1,0:T(8,128)S(1)} %multiply_add_fusion), kind=kOutput, calls=%fused_computation.6 | convolution fusion | flops 8158740480 | bytes 28313088 | tf_op jit(solution)/shard_map/kmix,qlm->iqkxl/dot_general | solution.py:19
  1062.5 14.8 copy.45
  1077.3 19.0 %reshape.298 = f32[32,12,4608]{2,1,0:T(8,128)} reshape(f32[4,8,12,96,48]{4,3,2,1,0:T(8,128)} %copy.45) | data formatting | bytes 14155776 | tf_op jit(solution)/shard_map/reshape | solution.py:104
  1096.3 142.4 %all-to-all-done.3 = f32[32,12,4608]{2,1,0:T(8,128)} async-done(((f32[32,12,4608]{2,1,0:T(8,128)}), f32[32,12,4608]{2,1,0:T(8,128)}, u32[]{:S(2)}, u32[]{:S(2)}) %all-to-all-start.3) | async-done | bytes 7077920 | tf_op jit(solution)/shard_map/all_to_all | solution.py:109
  1250.6 199.0 %all-to-all-done.2 = f32[32,12,4608]{2,1,0:T(8,128)} async-done(((f32[32,12,4608]{2,1,0:T(8,128)}), f32[32,12,4608]{2,1,0:T(8,128)}, u32[]{:S(2)}, u32[]{:S(2)}) %all-to-all-start.2) | async-done | bytes 7077920 | tf_op jit(solution)/shard_map/all_to_all | solution.py:108
  1457.8 24.1 %fusion.23 = f32[4608,384]{1,0:T(8,128)S(1)} fusion(f32[384,4608]{1,0:T(8,128)} %reshape.251, f32[384,4608]{1,0:T(8,128)} %reshape.253), kind=kOutput, calls=%fused_computation.39 | convolution fusion | flops 8156823552 | bytes 21233664 | tf_op jit(solution)/shard_map/ka,kz->az/dot_general | solution.py:19
  1481.9 18.6 %fusion.4 = f32[4608,384]{1,0:T(8,128)S(1)} fusion(f32[4608,384]{1,0:T(8,128)S(1)} %fusion.23, f32[384,4608]{1,0:T(8,128)S(1)} %copy-done.1), kind=kOutput, calls=%fused_computation.15 | convolution fusion | flops 8160509952 | bytes 21233664 | tf_op jit(solution)/shard_map/ka,kz->az/dot_general | solution.py:19
  1500.6 22.3 %divide_clamp_fusion = f32[4608,384]{1,0:T(8,128)} fusion(f32[4608,384]{1,0:T(8,128)S(1)} %fusion.4, f32[4608,384]{1,0:T(8,128)S(1)} %fusion.23, f32[384,4608]{1,0:T(8,128)S(1)} %bitcast.314), kind=kOutput, calls=%fused_computation.38 | convolution fusion | flops 8162279424 | bytes 28311552 | tf_op jit(solution)/shard_map/ka,kz->az/dot_general | solution.py:19
  (88 shorter events, 89.7 us)
Async XLA Ops:
  226.1 25.1 %copy-start.6 = (f32[4608,384]{1,0:T(8,128)S(1)}, f32[4608,384]{1,0:T(8,128)}, u32[]{:S(2)}) copy-start(f32[4608,384]{1,0:T(8,128)} %reshape.245) | copy-start | bytes 21233668
  251.1 20.5 %copy-start.3 = (f32[384,4608]{1,0:T(8,128)}, f32[384,4608]{1,0:T(8,128)S(1)}, u32[]{:S(2)}) copy-start(f32[384,4608]{1,0:T(8,128)S(1)} %fusion.29) | copy-start | bytes 21233668
  281.1 160.5 %all-to-all-start.1 = ((f32[32,1,12,4608]{3,1,2,0:T(1,128)}), f32[32,1,12,4608]{3,1,2,0:T(1,128)}, u32[]{:S(2)}, u32[]{:S(2)}) async-start(f32[32,1,12,4608]{3,1,2,0:T(1,128)} %copy.18), calls=%async_computation.1 | async-start | bytes 14155776 | tf_op jit(solution)/shard_map/all_to_all | solution.py:14
  441.6 211.2 %all-to-all-start = ((f32[32,12,4608]{2,1,0:T(8,128)}), f32[32,12,4608]{2,1,0:T(8,128)}, u32[]{:S(2)}, u32[]{:S(2)}) async-start(f32[32,12,4608]{2,1,0:T(8,128)} %reshape.247), calls=%async_computation | async-start | bytes 18874368 | tf_op jit(solution)/shard_map/all_to_all | solution.py:88
  678.6 26.6 %copy-start = (f32[12,4,8,96,48]{4,3,2,1,0:T(8,128)S(1)}, f32[12,4,8,96,48]{4,3,2,1,0:T(8,128)}, u32[]{:S(2)}) copy-start(f32[12,4,8,96,48]{4,3,2,1,0:T(8,128)} %reshape.248) | copy-start | bytes 21233668
  755.7 25.3 %copy-start.7 = (f32[12,4,96,384,1]{3,2,4,1,0:T(8,128)S(1)}, f32[12,4,96,384,1]{3,2,4,1,0:T(8,128)}, u32[]{:S(2)}) copy-start(f32[12,4,96,384,1]{3,2,4,1,0:T(8,128)} %fusion) | copy-start | bytes 21233668
  755.7 96.9 %slice-start = ((s8[7077888]{0:T(1024)(128)(4,1)}), s8[4194304]{0:T(1024)(128)(4,1)S(1)}, s32[]{:S(2)}) async-start(s8[7077888]{0:T(1024)(128)(4,1)} %bitcast.311), calls=%async_computation.4 | async-start | bytes 8388608
  781.0 51.0 %copy-start.9 = (f32[12,384,384,1]{2,1,3,0:T(8,128)}, f32[12,384,384,1]{2,1,3,0:T(8,128)S(1)}, u32[]{:S(2)}) copy-start(f32[12,384,384,1]{2,1,3,0:T(8,128)S(1)} %fusion.27) | copy-start | bytes 21233668
  781.0 71.5 %slice-start.1 = ((s8[7077888]{0:T(1024)(128)(4,1)}), s8[2883584]{0:T(1024)(128)(4,1)S(1)}, s32[]{:S(2)}) async-start(s8[7077888]{0:T(1024)(128)(4,1)} %bitcast.311), calls=%async_computation.5 | async-start | bytes 5767168
  903.1 3.0 copy-start.8
  920.8 44.2 %copy-start.2 = (f32[12,384,4,96]{1,3,2,0:T(8,128)}, f32[12,384,4,96]{1,3,2,0:T(8,128)S(1)}, u32[]{:S(2)}) copy-start(f32[12,384,4,96]{1,3,2,0:T(8,128)S(1)} %fusion.13) | copy-start | bytes 21233668
  940.7 24.3 %copy-start.5 = (f32[12,384,4,96]{1,3,2,0:T(8,128)}, f32[12,384,4,96]{1,3,2,0:T(8,128)S(1)}, u32[]{:S(2)}) copy-start(f32[12,384,4,96]{1,3,2,0:T(8,128)S(1)} %fusion.9) | copy-start | bytes 21233668
  965.0 3.7 copy-start.4
  1027.5 211.1 %all-to-all-start.3 = ((f32[32,12,4608]{2,1,0:T(8,128)}), f32[32,12,4608]{2,1,0:T(8,128)}, u32[]{:S(2)}, u32[]{:S(2)}) async-start(f32[32,12,4608]{2,1,0:T(8,128)} %reshape.299), calls=%async_computation.3 | async-start | bytes 18874368 | tf_op jit(solution)/shard_map/all_to_all | solution.py:109
  1238.7 211.0 %all-to-all-start.2 = ((f32[32,12,4608]{2,1,0:T(8,128)}), f32[32,12,4608]{2,1,0:T(8,128)}, u32[]{:S(2)}, u32[]{:S(2)}) async-start(f32[32,12,4608]{2,1,0:T(8,128)} %reshape.298), calls=%async_computation.2 | async-start | bytes 18874368 | tf_op jit(solution)/shard_map/all_to_all | solution.py:108
  1457.8 24.1 %copy-start.1 = (f32[384,4608]{1,0:T(8,128)S(1)}, f32[384,4608]{1,0:T(8,128)}, u32[]{:S(2)}) copy-start(f32[384,4608]{1,0:T(8,128)} %reshape.251) | copy-start | bytes 21233668
  1457.8 42.7 %slice-start.2 = ((s8[7077888]{0:T(1024)(128)(4,1)}), s8[4194304]{0:T(1024)(128)(4,1)S(1)}, s32[]{:S(2)}) async-start(s8[7077888]{0:T(1024)(128)(4,1)} %bitcast.313), calls=%async_computation.6 | async-start | bytes 8388608
  1481.9 18.6 %slice-start.3 = ((s8[7077888]{0:T(1024)(128)(4,1)}), s8[2883584]{0:T(1024)(128)(4,1)S(1)}, s32[]{:S(2)}) async-start(s8[7077888]{0:T(1024)(128)(4,1)} %bitcast.313), calls=%async_computation.7 | async-start | bytes 5767168
